TPU v7x, 32 devices: a whole 2x2x4 slice. The times are simulated.
32 devices in a mesh: dp: 2 (over core), seq: 4 (over y, x), tensor: 4 (over z).
Axes of the slice: x: 2, y: 2, z: 4, core: 2. Of those that a mesh axis runs over, the one named last changes fastest.
Arguments:
- tokens: bfloat16 [2, 2048, 2048], P('dp', ('seq', 'tensor')), may hold values from -6 to 6
- attn_gain: float32 [2048], replicated, may hold values from 0.5 to 1.5
- w_qkv: bfloat16 [3, 2048, 2048], P(None, None, 'tensor'), may hold values from -1 to 1
- w_out: bfloat16 [2048, 2048], P('tensor'), may hold values from -0.125 to 0.125
- mlp_gain: float32 [2048], replicated, may hold values from 0.5 to 1.5
- w_up: bfloat16 [2048, 8192], P(None, 'tensor'), may hold values from -0.125 to 0.125
- w_down: bfloat16 [8192, 2048], P('tensor'), may hold values from -0.0625 to 0.0625
- pool_gain: float32 [2048], replicated, may hold values from -8 to 8
- pool_bias: float32 [2048], replicated, may hold values from 0.5 to 5
- value_weight: float32 [2048], replicated, may hold values from -6 to 6
- valid_frames: int32 [2], replicated, may hold values from 4 to 8, as said below
Outputs:
- hidden: bfloat16 [2, 2048, 2048], P('dp', ('seq', 'tensor'))
- frame_values: float32 [2, 8], P('dp', 'seq')
- advantages: float32 [2, 8], P('dp', 'seq')
Inputs may be any that keep to these rules, and one draw needn't show every extreme that they name: `valid_frames`: at least one rollout keeps all 8 frames and at least one keeps 8 // 2 of them.
All inputs are finite; a program needn't handle non-finite values.
Results may differ from a plain program's by a relative error of at most 0.017.
Values may be sent and summed in bfloat16 or wider, within the bound.
A program may use at most 256 MiB of HBM per device.

v0:
```python
import jax
import jax.numpy as jnp
from jax import lax
from jax.sharding import PartitionSpec as P

HEAD_DIM = 128
TOK_FRAME = 256
FR_DEV = 2


def entering_2(value, axis, join, neutral):
    count, mine = (lax.axis_size(axis), lax.axis_index(axis))
    pieces = jax.tree.map(lambda part: lax.all_gather(part, axis), value)
    subtotal = jax.tree.map(
        lambda part, zero: jnp.full_like(part, 0) + jnp.asarray(zero, part.dtype), value, neutral
    )

    def turn(position, subtotal):
        longer = join(subtotal, jax.tree.map(lambda part: part[position], pieces))
        return jax.tree.map(lambda new, old: jnp.where(position < mine, new, old), longer, subtotal)

    return lax.fori_loop(0, count - 1, turn, subtotal)


def rms_norm(values, gain):
    floats = values.astype(jnp.float32)
    square = jnp.mean(floats * floats, axis=-1, keepdims=True)
    return (floats * lax.rsqrt(square + 1e-05) * gain).astype(jnp.bfloat16)


def compose(earlier, later):
    return (earlier[0] * later[0], later[0] * earlier[1] + later[1])


def local(
    tokens,
    attn_gain,
    w_qkv,
    w_out,
    mlp_gain,
    w_up,
    w_down,
    pool_gain,
    pool_bias,
    value_weight,
    valid_frames,
):
    rows = tokens[0]
    row_count = rows.shape[0]
    seq_index = lax.axis_index("seq")
    tensor_index = lax.axis_index("tensor")
    roll_index = lax.axis_index("dp")
    length = valid_frames[roll_index]
    local_heads = w_qkv.shape[2] // HEAD_DIM
    scale = 1.0 / HEAD_DIM**0.5
    block_tokens = lax.all_gather(rows, "tensor", axis=0, tiled=True)
    qkv = jnp.einsum(
        "nd,cde->nce", rms_norm(block_tokens, attn_gain), w_qkv, preferred_element_type=jnp.float32
    ).astype(jnp.bfloat16)
    block = qkv.shape[0]
    query = qkv[:, 0].reshape(block, local_heads, HEAD_DIM)
    query_frame = (seq_index * block + jnp.arange(block, dtype=jnp.int32)) // TOK_FRAME
    peak = jnp.full((local_heads, block), -1e30, jnp.float32)
    key_piece = lax.all_gather(qkv[:, 1], "seq", axis=0, tiled=True)
    value_piece = lax.all_gather(qkv[:, 2], "seq", axis=0, tiled=True)
    width = key_piece.shape[0]
    key_heads = key_piece.reshape(width, local_heads, HEAD_DIM)
    value_heads = value_piece.reshape(width, local_heads, HEAD_DIM)
    scores = (
        jnp.einsum("qhe,khe->hqk", query, key_heads, preferred_element_type=jnp.float32) * scale
    )
    key_frame = jnp.arange(width, dtype=jnp.int32) // TOK_FRAME
    allowed = (key_frame[None, :] <= query_frame[:, None]) & (key_frame[None, :] < length)
    scores = jnp.where(allowed[None], scores, -1e30)
    new_peak = jnp.maximum(peak, jnp.max(scores, axis=-1))
    weights = jnp.where(allowed[None], jnp.exp(scores - new_peak[..., None]), 0.0)
    total = jnp.sum(weights, axis=-1)
    acc = jnp.einsum(
        "hqk,khe->hqe",
        weights.astype(jnp.bfloat16),
        value_heads,
        preferred_element_type=jnp.float32,
    )
    peak, total, acc = (new_peak, total, acc)
    mixed = (
        (acc / total[..., None])
        .transpose(1, 0, 2)
        .reshape(block, local_heads * HEAD_DIM)
        .astype(jnp.bfloat16)
    )
    attn_sum = lax.psum(
        jnp.dot(mixed, w_out, preferred_element_type=jnp.float32).astype(jnp.bfloat16), "tensor"
    ).astype(jnp.float32)
    after_attn = (block_tokens.astype(jnp.float32) + attn_sum).astype(jnp.bfloat16)
    up = jax.nn.gelu(
        jnp.dot(rms_norm(after_attn, mlp_gain), w_up, preferred_element_type=jnp.float32),
        approximate=True,
    ).astype(jnp.bfloat16)
    own_after = lax.dynamic_slice_in_dim(after_attn, tensor_index * row_count, row_count, 0)
    down_sum = lax.psum_scatter(
        jnp.dot(up, w_down, preferred_element_type=jnp.float32).astype(jnp.bfloat16),
        "tensor",
        scatter_dimension=0,
        tiled=True,
    ).astype(jnp.float32)
    hidden = (own_after.astype(jnp.float32) + down_sum).astype(jnp.bfloat16)
    local_frame = (tensor_index * row_count + jnp.arange(row_count, dtype=jnp.int32)) // TOK_FRAME
    selector = (local_frame[None, :] == jnp.arange(FR_DEV, dtype=jnp.int32)[:, None]).astype(
        jnp.bfloat16
    )
    sums = jnp.dot(selector, hidden, preferred_element_type=jnp.float32)
    sums = lax.psum(sums, "tensor")
    gain, offset, head_weight = (pool_gain, pool_bias, value_weight)
    means = sums / TOK_FRAME
    frame_global = seq_index * FR_DEV + jnp.arange(FR_DEV, dtype=jnp.int32)
    valid = frame_global < length
    gate = jax.nn.sigmoid(means * gain + offset)
    decay = jnp.where(valid[:, None], gate, 1.0)
    source = jnp.where(valid[:, None], (1.0 - gate) * means, 0.0)
    agg_decay = jnp.ones_like(means[0])
    agg_source = jnp.zeros_like(means[0])
    for frame in range(FR_DEV):
        agg_decay, agg_source = compose((agg_decay, agg_source), (decay[frame], source[frame]))
    entering = entering_2(
        (agg_decay, agg_source),
        "seq",
        compose,
        (jnp.ones_like(agg_decay), jnp.zeros_like(agg_source)),
    )
    state = entering[1]
    collected = []
    for frame in range(FR_DEV):
        state = decay[frame] * state + source[frame]
        collected.append(jnp.sum(state * head_weight))
    partial_values = jnp.stack(collected)
    values = jnp.where(valid, partial_values, 0.0)
    pick = jnp.sum(jnp.where(frame_global == length - 1, values, 0.0))
    count = jnp.sum(valid_frames).astype(jnp.float32)
    slot = (jnp.arange(lax.axis_size("dp"), dtype=jnp.int32) == roll_index).astype(jnp.float32)
    entries = jnp.stack([pick, jnp.sum(values), jnp.sum(values * values)])
    table = lax.psum(entries[:, None] * slot[None, :], ("dp", "seq"))
    finals, first_sums, second_sums = (table[0], table[1], table[2])
    lengths = valid_frames.astype(jnp.float32)
    mean = jnp.sum(lengths * finals - first_sums) / count
    squares = jnp.sum(lengths * finals * finals - 2.0 * finals * first_sums + second_sums) / count
    variance = squares - mean * mean
    final = jnp.sum(finals * slot)
    gap = jnp.where(valid, final - values, 0.0)
    centered = jnp.where(valid, gap - mean, 0.0)
    advantages = jnp.where(valid, centered * lax.rsqrt(variance + 1e-05), 0.0)
    return (hidden[None], values[None], advantages[None])


def solution(mesh):
    in_specs = (
        P("dp", ("seq", "tensor"), None),
        P(),
        P(None, None, "tensor"),
        P("tensor", None),
        P(),
        P(None, "tensor"),
        P("tensor", None),
        P(),
        P(),
        P(),
        P(),
    )
    out_specs = (P("dp", ("seq", "tensor"), None), P("dp", "seq"), P("dp", "seq"))
    return jax.shard_map(local, mesh=mesh, in_specs=in_specs, out_specs=out_specs, check_vma=False)
```

profile of v0, /device:TPU:1, one launch (start us, length us, event | category | flops | bytes accessed | tf_op | source)
XLA Modules:
  0.0 369.2 jit_solution(14914907635023550377)
XLA Ops:
  7.2 0.7 all-gather.9.cloned.1.call-update
  8.0 49.2 %all-gather.9.cloned.1.call-done = bf16[1,512,2048]{2,1,0:T(8,128)(2,1)} async-done(((bf16[1,128,2048]{2,1,0:T(8,128)(2,1)}), bf16[1,512,2048]{2,1,0:T(8,128)(2,1)}) %all-gather.9.cloned.1.call-update) | async-done | bytes 2097168 | tf_op jit(solution)/shard_map/all_gather | solution.py:56
  57.1 2.1 fusion.17
  59.2 7.1 %fusion.36 = bf16[512,3,512]{0,2,1:T(8,128)(2,1)S(1)} fusion(bf16[3,2048,512]{2,1,0:T(8,128)(2,1)} %param.15, bf16[1,512,2048]{2,1,0:T(8,128)(2,1)} %all-gather.9.cloned.1.call-done, f32[2048]{0:T(1024)} %param.14, f32[512]{0:T(512)S(1)} %add_rsqrt_fusion.1), kind=kOutput, calls=%fused_computation.46 | convolution fusion | flops 3226206208 | bytes 9971712 | tf_op jit(solution)/shard_map/nd,cde->nce/dot_general | solution.py:57
  66.3 1.2 fusion.70
  67.6 0.7 dynamic_slice.20
  68.5 0.6 broadcast_compare_fusion
  69.2 0.7 compare_and_fusion
  69.9 31.6 %all-gather.11.cloned.1.call-done = bf16[2048,1,512]{0,2,1:T(8,128)(2,1)} async-done(((bf16[512,1,512]{0,2,1:T(8,128)(2,1)}), bf16[2048,1,512]{0,2,1:T(8,128)(2,1)}) %all-gather.11.cloned.1.call-update) | async-done | bytes 2097168 | tf_op jit(solution)/shard_map/all_gather | solution.py:64
  101.6 5.2 %fusion = (f32[4,512]{1,0:T(4,128)S(1)}, f32[4,512,2048]{2,1,0:T(8,128)S(1)}) fusion(pred[512,2048]{1,0:T(8,128)(4,1)S(1)} %compare_and_fusion, bf16[512,4,128]{0,2,1:T(8,128)(2,1)} %bitcast.94, bf16[2048,4,128]{0,2,1:T(8,128)(2,1)} %bitcast.93), kind=kOutput, calls=%fused_computation.5 | convolution fusion | flops 1086322688 | bytes 20455424 | tf_op jit(solution)/shard_map/qhe,khe->hqk/dot_general | solution.py:70
  106.8 6.0 %copy-done.1 = f32[4,512,2048]{2,1,0:T(8,128)} copy-done((f32[4,512,2048]{2,1,0:T(8,128)}, f32[4,512,2048]{2,1,0:T(8,128)S(1)}, u32[]{:S(2)}) %copy-start.1) | copy-done | bytes 16777240
  112.9 5.0 %fusion.1 = f32[4,512]{1,0:T(4,128)S(1)} fusion(f32[4,512,2048]{2,1,0:T(8,128)S(1)} %get-tuple-element.152, f32[4,512]{1,0:T(4,128)S(1)} %broadcast_maximum_fusion, pred[512,2048]{1,0:T(8,128)(4,1)S(1)} %compare_and_fusion), kind=kLoop, calls=%fused_computation.6 | loop fusion | flops 20969472 | bytes 17842176 | tf_op jit(solution)/shard_map/reduce_sum | solution.py:77
  117.9 20.6 %all-gather.13.cloned.1.call-done = bf16[2048,1,512]{0,2,1:T(8,128)(2,1)} async-done(((bf16[512,1,512]{0,2,1:T(8,128)(2,1)}), bf16[2048,1,512]{0,2,1:T(8,128)(2,1)}) %all-gather.13.cloned.1.call-update) | async-done | bytes 2097168 | tf_op jit(solution)/shard_map/all_gather | solution.py:65
  138.5 8.7 %divide_convert_fusion = bf16[512,4,128]{0,2,1:T(8,128)(2,1)S(1)} fusion(bf16[2048,4,128]{0,2,1:T(8,128)(2,1)} %bitcast.104, f32[4,512,2048]{2,1,0:T(8,128)} %copy-done.1, f32[4,512]{1,0:T(4,128)S(1)} %broadcast_maximum_fusion, pred[512,2048]{1,0:T(8,128)(4,1)S(1)} %compare_and_fusion, f32[512,4]{0,1:T(4,128)S(1)} %bitcast.103), kind=kOutput, calls=%fused_computation.49 | convolution fusion | flops 1095237632 | bytes 20463616 | tf_op jit(solution)/shard_map/hqk,khe->hqe/dot_general | solution.py:78
  147.2 2.6 convolution_convert_fusion.1
  150.2 85.9 %all-reduce.2.cloned.1.call-done = bf16[512,2048]{1,0:T(8,128)(2,1)} async-done(((bf16[512,2048]{1,0:T(8,128)(2,1)}), bf16[512,2048]{1,0:T(8,128)(2,1)}) %all-reduce.2.cloned.1.call-update) | async-done | bytes 2097168 | tf_op jit(solution)/shard_map/psum | solution.py:91
  236.0 4.5 %fusion.6 = (f32[512]{0:T(512)S(1)}, bf16[512,2048]{1,0:T(8,128)(2,1)}) fusion(bf16[512,2048]{1,0:T(8,128)(2,1)} %all-reduce.2.cloned.1.call-done, bf16[1,512,2048]{2,1,0:T(8,128)(2,1)} %all-gather.9.cloned.1.call-done), kind=kLoop, calls=%fused_computation.16 | loop fusion | flops 7339520 | bytes 6293504 | tf_op jit(solution)/shard_map/reduce_sum | solution.py:27
  240.6 16.6 %convolution_convert_fusion = bf16[512,2048]{1,0:T(8,128)(2,1)} fusion(bf16[2048,2048]{1,0:T(8,128)(2,1)} %param.19, bf16[2048,2048]{1,0:T(8,128)(2,1)} %param.18, bf16[512,2048]{1,0:T(8,128)(2,1)} %get-tuple-element.139, f32[2048]{0:T(1024)S(1)} %copy-done.6, f32[512]{0:T(512)S(1)} %add_rsqrt_fusion), kind=kOutput, calls=%fused_computation.32 | convolution fusion | flops 8604614656 | bytes 20981760 | tf_op jit(solution)/shard_map/dot_general | solution.py:101
  257.2 0.6 reduce_sum.118
  258.5 0.6 fusion.60
  259.2 40.8 %reduce-scatter.2.cloned.1.call-done = bf16[128,2048]{1,0:T(8,128)(2,1)} async-done(((bf16[512,2048]{1,0:T(8,128)(2,1)}), bf16[128,2048]{1,0:T(8,128)(2,1)}) %reduce-scatter.2.cloned.1.call-update) | async-done | bytes 524304 | tf_op jit(solution)/shard_map/reduce_scatter | solution.py:100
  300.0 1.4 fusion.44
  301.4 14.0 %psum.22 = f32[2,2048]{1,0:T(2,128)S(1)} all-reduce(f32[2,2048]{1,0:T(2,128)S(1)} %fusion.44), channel_id=1, replica_groups=mesh['dp'=2,'seq'=4,'tensor'=4] {'tensor'}, use_global_device_ids=true, to_apply=%region_6.7 | all-reduce | flops 4096 | bytes 32768 | tf_op jit(solution)/shard_map/psum | solution.py:112
  315.5 5.8 %all-gather.4 = f32[4,1,2048]{2,1,0:T(1,128)S(1)} all-gather(f32[1,1,2048]{2,1,0:T(1,128)S(1)} %get-tuple-element.147), channel_id=1, replica_groups=mesh['dp'=2,'seq'=4,'tensor'=4] {'seq'}, dimensions={0}, use_global_device_ids=true | all-gather | bytes 40960 | tf_op jit(solution)/shard_map/all_gather | solution.py:13
  321.4 6.1 %all-gather.3 = f32[4,1,2048]{2,1,0:T(1,128)S(1)} all-gather(f32[1,1,2048]{2,1,0:T(1,128)S(1)} %get-tuple-element.146), channel_id=1, replica_groups=mesh['dp'=2,'seq'=4,'tensor'=4] {'seq'}, dimensions={0}, use_global_device_ids=true | all-gather | bytes 40960 | tf_op jit(solution)/shard_map/all_gather | solution.py:13
  327.7 0.6 multiply_reduce_fusion.1
  328.3 2.6 fusion.55
  330.9 2.0 pad_maximum_fusion
  333.5 21.9 %psum.23 = f32[3,2]{1,0:T(4,128)S(1)} all-reduce(f32[3,2]{1,0:T(4,128)S(1)} %broadcast_multiply_fusion.1), channel_id=1, replica_groups=mesh['dp'=2,'seq'=4,'tensor'=4] {'dp','seq'}, use_global_device_ids=true, to_apply=%region_14.15 | all-reduce | flops 6 | bytes 48 | tf_op jit(solution)/shard_map/psum | solution.py:141
  355.4 0.6 fusion.57
  357.4 3.1 multiply_select_fusion.2
  360.5 2.1 fusion.45
  (44 shorter events, 1.3 us)
Async XLA Ops:
  7.2 140.0 %copy-start = (bf16[512,2048]{1,0:T(8,128)(2,1)S(1)}, bf16[512,2048]{1,0:T(8,128)(2,1)}, u32[]{:S(2)}) copy-start(bf16[512,2048]{1,0:T(8,128)(2,1)} %param.16) | copy-start | bytes 6291460
  7.2 50.0 %all-gather.9.cloned.1.call-start = ((), (), s32[]{:S(2)}) async-start(), calls=%async_computation.3 | async-start | bytes 2621440 | tf_op jit(solution)/shard_map/all_gather | solution.py:56
  7.9 93.6 %all-gather.11.cloned.1.call-start = ((), (), s32[]{:S(2)}) async-start(), calls=%async_computation.4 | async-start | bytes 2621440 | tf_op jit(solution)/shard_map/all_gather | solution.py:64
  59.2 8.4 %copy-start.5 = (s32[2]{0:T(128)S(1)}, s32[2]{0:T(128)}, u32[]{:S(2)}) copy-start(s32[2]{0:T(128)} %param.23) | copy-start | bytes 28
  67.5 70.9 %all-gather.13.cloned.1.call-start = ((), (), s32[]{:S(2)}) async-start(), calls=%async_computation.5 | async-start | bytes 2621440 | tf_op jit(solution)/shard_map/all_gather | solution.py:65
  68.3 167.7 %all-reduce.2.cloned.1.call-start = ((), (), s32[]{:S(2)}) async-start(), calls=%async_computation.1 | async-start | bytes 4194304 | tf_op jit(solution)/shard_map/psum | solution.py:91
  106.8 6.1 %copy-start.1 = (f32[4,512,2048]{2,1,0:T(8,128)}, f32[4,512,2048]{2,1,0:T(8,128)S(1)}, u32[]{:S(2)}) copy-start(f32[4,512,2048]{2,1,0:T(8,128)S(1)} %get-tuple-element.152) | copy-start | bytes 50331652
  149.9 90.7 %copy-start.6 = (f32[2048]{0:T(1024)S(1)}, f32[2048]{0:T(1024)}, u32[]{:S(2)}) copy-start(f32[2048]{0:T(1024)} %param.17) | copy-start | bytes 24580
  149.9 150.1 %reduce-scatter.2.cloned.1.call-start = ((), (), s32[]{:S(2)}) async-start(), calls=%async_computation.2 | async-start | bytes 2621440 | tf_op jit(solution)/shard_map/reduce_scatter | solution.py:100
  240.6 18.6 %copy-start.3 = (f32[2048]{0:T(1024)S(1)}, f32[2048]{0:T(1024)}, u32[]{:S(2)}) copy-start(f32[2048]{0:T(1024)} %param.20) | copy-start | bytes 24580
  240.6 74.8 %copy-start.4 = (f32[2048]{0:T(1024)S(1)}, f32[2048]{0:T(1024)}, u32[]{:S(2)}) copy-start(f32[2048]{0:T(1024)} %param.21) | copy-start | bytes 24580
  257.2 70.5 %copy-start.2 = (f32[2048]{0:T(1024)S(1)}, f32[2048]{0:T(1024)}, u32[]{:S(2)}) copy-start(f32[2048]{0:T(1024)} %param.22) | copy-start | bytes 24580
Sparse Core Ops, SparseCore 0:
  9.6 47.5 all-gather.8
  67.7 33.8 all-gather.10
  103.4 35.0 all-gather.12
  150.0 85.9 all-reduce.1
  257.3 42.5 reduce-scatter.1
where the time goes:
time: 370 us; the launch traced here: 369 us
  waiting for transfers between devices  229 us (62%)
  blocking collectives  47.8 us (13%)
  matrix products  41.7 us (11%)
  other arithmetic  25.7 us (7%)
  between operations  16.5 us (4%)
  local copies, waits for them, and re-layouts  7.99 us (2%)
    psum x1, waiting for transfers between devices, local(): lax.psum(jnp.dot(mixed, w_out, preferred_element_type=jnp.float32).astype...  85.9 us
    all_gather x1, waiting for transfers between devices, local(): block_tokens = lax.all_gather(rows, 'tensor', axis=0, tiled=True)  49.2 us
    reduce_scatter x1, waiting for transfers between devices, local(): lax.psum_scatter(jnp.dot(up, w_down, preferred_element_type=jnp.float32)....  40.8 us
    all_gather x1, waiting for transfers between devices, local(): key_piece = lax.all_gather(qkv[:, 1], 'seq', axis=0, tiled=True)  31.6 us
    psum x1, blocking collectives, local(): table = lax.psum(entries[:, None] * slot[None, :], ('dp', 'seq'))  21.9 us
    all_gather x1, waiting for transfers between devices, local(): value_piece = lax.all_gather(qkv[:, 2], 'seq', axis=0, tiled=True)  20.6 us
    dot_general x1, matrix products, local(): jnp.dot(up, w_down, preferred_element_type=jnp.float32).astype(jnp.bfloat16)  16.6 us
    psum x1, blocking collectives, local(): sums = lax.psum(sums, 'tensor')  14 us
  transfers between devices with their start and end apart: 5, of which 5 were waited for; matrix products, arithmetic and copies ran while one was open for 4% of the time, Pallas kernels for 0%

commit v1 on v0

--- a/solution.py
+++ b/solution.py
@@ -138,7 +138,7 @@
     count = jnp.sum(valid_frames).astype(jnp.float32)
     slot = (jnp.arange(lax.axis_size("dp"), dtype=jnp.int32) == roll_index).astype(jnp.float32)
     entries = jnp.stack([pick, jnp.sum(values), jnp.sum(values * values)])
-    table = lax.psum(entries[:, None] * slot[None, :], ("dp", "seq"))
+    table = lax.psum(lax.psum(entries[:, None] * slot[None, :], "dp"), "seq")
     finals, first_sums, second_sums = (table[0], table[1], table[2])
     lengths = valid_frames.astype(jnp.float32)
     mean = jnp.sum(lengths * finals - first_sums) / count

time: 370 us -> 368 us (level)
  blocking collectives: 47.8 us -> 43.3 us
    psum x1 -> x2, blocking collectives: 21.9 us -> 17.5 us  [local(): table = lax.psum(lax.psum(entries[:, None] * slot[None, :], 'dp'), 'seq')]
where the time goes in v1:
time: 368 us; the launch traced here: 365 us
  waiting for transfers between devices  229 us (62%)
  blocking collectives  43.3 us (12%)
  matrix products  41.7 us (11%)
  other arithmetic  25.7 us (7%)
  between operations  16.6 us (5%)
  local copies, waits for them, and re-layouts  7.99 us (2%)
    psum x1, waiting for transfers between devices, local(): lax.psum(jnp.dot(mixed, w_out, preferred_element_type=jnp.float32).astype...  85.9 us
    all_gather x1, waiting for transfers between devices, local(): block_tokens = lax.all_gather(rows, 'tensor', axis=0, tiled=True)  49.2 us
    reduce_scatter x1, waiting for transfers between devices, local(): lax.psum_scatter(jnp.dot(up, w_down, preferred_element_type=jnp.float32)....  41.4 us
    all_gather x1, waiting for transfers between devices, local(): key_piece = lax.all_gather(qkv[:, 1], 'seq', axis=0, tiled=True)  31.6 us
    all_gather x1, waiting for transfers between devices, local(): value_piece = lax.all_gather(qkv[:, 2], 'seq', axis=0, tiled=True)  20.6 us
    psum x2, blocking collectives, local(): table = lax.psum(lax.psum(entries[:, None] * slot[None, :], 'dp'), 'seq')  17.5 us
    dot_general x1, matrix products, local(): jnp.dot(up, w_down, preferred_element_type=jnp.float32).astype(jnp.bfloat16)  16.6 us
    psum x1, blocking collectives, local(): sums = lax.psum(sums, 'tensor')  14 us
  transfers between devices with their start and end apart: 5, of which 5 were waited for; matrix products, arithmetic and copies ran while one was open for 4% of the time, Pallas kernels for 0%

profile of v1, /device:TPU:1, one launch (start us, length us, event | category | flops | bytes accessed | tf_op | source)
XLA Modules:
  0.0 365.4 jit_solution(4076076993267411949)
XLA Ops:
  7.2 0.7 all-gather.9.cloned.1.call-update
  8.0 49.2 %all-gather.9.cloned.1.call-done = bf16[1,512,2048]{2,1,0:T(8,128)(2,1)} async-done(((bf16[1,128,2048]{2,1,0:T(8,128)(2,1)}), bf16[1,512,2048]{2,1,0:T(8,128)(2,1)}) %all-gather.9.cloned.1.call-update) | async-done | bytes 2097168 | tf_op jit(solution)/shard_map/all_gather | solution.py:56
  57.1 2.1 fusion.17
  59.2 7.1 %fusion.36 = bf16[512,3,512]{0,2,1:T(8,128)(2,1)S(1)} fusion(bf16[3,2048,512]{2,1,0:T(8,128)(2,1)} %param.15, bf16[1,512,2048]{2,1,0:T(8,128)(2,1)} %all-gather.9.cloned.1.call-done, f32[2048]{0:T(1024)} %param.14, f32[512]{0:T(512)S(1)} %add_rsqrt_fusion.1), kind=kOutput, calls=%fused_computation.46 | convolution fusion | flops 3226206208 | bytes 9971712 | tf_op jit(solution)/shard_map/nd,cde->nce/dot_general | solution.py:57
  66.3 1.2 fusion.70
  67.6 0.7 dynamic_slice.20
  68.5 0.6 broadcast_compare_fusion
  69.2 0.7 compare_and_fusion
  69.9 31.6 %all-gather.11.cloned.1.call-done = bf16[2048,1,512]{0,2,1:T(8,128)(2,1)} async-done(((bf16[512,1,512]{0,2,1:T(8,128)(2,1)}), bf16[2048,1,512]{0,2,1:T(8,128)(2,1)}) %all-gather.11.cloned.1.call-update) | async-done | bytes 2097168 | tf_op jit(solution)/shard_map/all_gather | solution.py:64
  101.6 5.2 %fusion = (f32[4,512]{1,0:T(4,128)S(1)}, f32[4,512,2048]{2,1,0:T(8,128)S(1)}) fusion(pred[512,2048]{1,0:T(8,128)(4,1)S(1)} %compare_and_fusion, bf16[512,4,128]{0,2,1:T(8,128)(2,1)} %bitcast.94, bf16[2048,4,128]{0,2,1:T(8,128)(2,1)} %bitcast.93), kind=kOutput, calls=%fused_computation.5 | convolution fusion | flops 1086322688 | bytes 20455424 | tf_op jit(solution)/shard_map/qhe,khe->hqk/dot_general | solution.py:70
  106.8 6.0 %copy-done.1 = f32[4,512,2048]{2,1,0:T(8,128)} copy-done((f32[4,512,2048]{2,1,0:T(8,128)}, f32[4,512,2048]{2,1,0:T(8,128)S(1)}, u32[]{:S(2)}) %copy-start.1) | copy-done | bytes 16777240
  112.9 5.0 %fusion.1 = f32[4,512]{1,0:T(4,128)S(1)} fusion(f32[4,512,2048]{2,1,0:T(8,128)S(1)} %get-tuple-element.152, f32[4,512]{1,0:T(4,128)S(1)} %broadcast_maximum_fusion, pred[512,2048]{1,0:T(8,128)(4,1)S(1)} %compare_and_fusion), kind=kLoop, calls=%fused_computation.6 | loop fusion | flops 20969472 | bytes 17842176 | tf_op jit(solution)/shard_map/reduce_sum | solution.py:77
  117.9 20.6 %all-gather.13.cloned.1.call-done = bf16[2048,1,512]{0,2,1:T(8,128)(2,1)} async-done(((bf16[512,1,512]{0,2,1:T(8,128)(2,1)}), bf16[2048,1,512]{0,2,1:T(8,128)(2,1)}) %all-gather.13.cloned.1.call-update) | async-done | bytes 2097168 | tf_op jit(solution)/shard_map/all_gather | solution.py:65
  138.5 8.7 %divide_convert_fusion = bf16[512,4,128]{0,2,1:T(8,128)(2,1)S(1)} fusion(bf16[2048,4,128]{0,2,1:T(8,128)(2,1)} %bitcast.104, f32[4,512,2048]{2,1,0:T(8,128)} %copy-done.1, f32[4,512]{1,0:T(4,128)S(1)} %broadcast_maximum_fusion, pred[512,2048]{1,0:T(8,128)(4,1)S(1)} %compare_and_fusion, f32[512,4]{0,1:T(4,128)S(1)} %bitcast.103), kind=kOutput, calls=%fused_computation.49 | convolution fusion | flops 1095237632 | bytes 20463616 | tf_op jit(solution)/shard_map/hqk,khe->hqe/dot_general | solution.py:78
  147.2 2.6 convolution_convert_fusion.1
  150.2 85.9 %all-reduce.2.cloned.1.call-done = bf16[512,2048]{1,0:T(8,128)(2,1)} async-done(((bf16[512,2048]{1,0:T(8,128)(2,1)}), bf16[512,2048]{1,0:T(8,128)(2,1)}) %all-reduce.2.cloned.1.call-update) | async-done | bytes 2097168 | tf_op jit(solution)/shard_map/psum | solution.py:91
  236.0 4.5 %fusion.6 = (f32[512]{0:T(512)S(1)}, bf16[512,2048]{1,0:T(8,128)(2,1)}) fusion(bf16[512,2048]{1,0:T(8,128)(2,1)} %all-reduce.2.cloned.1.call-done, bf16[1,512,2048]{2,1,0:T(8,128)(2,1)} %all-gather.9.cloned.1.call-done), kind=kLoop, calls=%fused_computation.16 | loop fusion | flops 7339520 | bytes 6293504 | tf_op jit(solution)/shard_map/reduce_sum | solution.py:27
  240.6 16.6 %convolution_convert_fusion = bf16[512,2048]{1,0:T(8,128)(2,1)} fusion(bf16[2048,2048]{1,0:T(8,128)(2,1)} %param.19, bf16[2048,2048]{1,0:T(8,128)(2,1)} %param.18, bf16[512,2048]{1,0:T(8,128)(2,1)} %get-tuple-element.139, f32[2048]{0:T(1024)S(1)} %copy-done.6, f32[512]{0:T(512)S(1)} %add_rsqrt_fusion), kind=kOutput, calls=%fused_computation.32 | convolution fusion | flops 8604614656 | bytes 20981760 | tf_op jit(solution)/shard_map/dot_general | solution.py:101
  257.9 0.6 fusion.60
  258.5 41.4 %reduce-scatter.2.cloned.1.call-done = bf16[128,2048]{1,0:T(8,128)(2,1)} async-done(((bf16[512,2048]{1,0:T(8,128)(2,1)}), bf16[128,2048]{1,0:T(8,128)(2,1)}) %reduce-scatter.2.cloned.1.call-update) | async-done | bytes 524304 | tf_op jit(solution)/shard_map/reduce_scatter | solution.py:100
  300.0 1.4 fusion.44
  301.4 14.0 %psum.29 = f32[2,2048]{1,0:T(2,128)S(1)} all-reduce(f32[2,2048]{1,0:T(2,128)S(1)} %fusion.44), channel_id=1, replica_groups=mesh['dp'=2,'seq'=4,'tensor'=4] {'tensor'}, use_global_device_ids=true, to_apply=%region_6.7 | all-reduce | flops 4096 | bytes 32768 | tf_op jit(solution)/shard_map/psum | solution.py:112
  315.5 5.8 %all-gather.4 = f32[4,1,2048]{2,1,0:T(1,128)S(1)} all-gather(f32[1,1,2048]{2,1,0:T(1,128)S(1)} %get-tuple-element.147), channel_id=1, replica_groups=mesh['dp'=2,'seq'=4,'tensor'=4] {'seq'}, dimensions={0}, use_global_device_ids=true | all-gather | bytes 40960 | tf_op jit(solution)/shard_map/all_gather | solution.py:13
  321.4 6.1 %all-gather.3 = f32[4,1,2048]{2,1,0:T(1,128)S(1)} all-gather(f32[1,1,2048]{2,1,0:T(1,128)S(1)} %get-tuple-element.146), channel_id=1, replica_groups=mesh['dp'=2,'seq'=4,'tensor'=4] {'seq'}, dimensions={0}, use_global_device_ids=true | all-gather | bytes 40960 | tf_op jit(solution)/shard_map/all_gather | solution.py:13
  328.3 2.6 fusion.55
  330.9 2.0 pad_maximum_fusion
  332.9 0.6 reduce_sum.118
  333.6 10.6 %psum.30 = f32[3,2]{1,0:T(4,128)S(1)} all-reduce(f32[3,2]{1,0:T(4,128)S(1)} %broadcast_multiply_fusion.1), channel_id=1, replica_groups=mesh['dp'=2,'seq'=4,'tensor'=4] {'dp'}, use_global_device_ids=true, to_apply=%region_14.15 | all-reduce | flops 6 | bytes 48 | tf_op jit(solution)/shard_map/psum | solution.py:141
  344.8 6.9 %psum.31 = f32[3,2]{1,0:T(4,128)S(1)} all-reduce(f32[3,2]{1,0:T(4,128)S(1)} %psum.30), channel_id=1, replica_groups=mesh['dp'=2,'seq'=4,'tensor'=4] {'seq'}, use_global_device_ids=true, to_apply=%region_15.16 | all-reduce | flops 6 | bytes 48 | tf_op jit(solution)/shard_map/psum | solution.py:141
  351.7 0.6 fusion.57
  353.7 3.1 multiply_select_fusion.2
  356.8 2.1 fusion.45
  (45 shorter events, 1.9 us)
Async XLA Ops:
  7.2 140.0 %copy-start = (bf16[512,2048]{1,0:T(8,128)(2,1)S(1)}, bf16[512,2048]{1,0:T(8,128)(2,1)}, u32[]{:S(2)}) copy-start(bf16[512,2048]{1,0:T(8,128)(2,1)} %param.16) | copy-start | bytes 6291460
  7.2 50.0 %all-gather.9.cloned.1.call-start = ((), (), s32[]{:S(2)}) async-start(), calls=%async_computation.3 | async-start | bytes 2621440 | tf_op jit(solution)/shard_map/all_gather | solution.py:56
  7.9 93.6 %all-gather.11.cloned.1.call-start = ((), (), s32[]{:S(2)}) async-start(), calls=%async_computation.4 | async-start | bytes 2621440 | tf_op jit(solution)/shard_map/all_gather | solution.py:64
  59.2 8.4 %copy-start.5 = (s32[2]{0:T(128)S(1)}, s32[2]{0:T(128)}, u32[]{:S(2)}) copy-start(s32[2]{0:T(128)} %param.23) | copy-start | bytes 28
  67.5 70.9 %all-gather.13.cloned.1.call-start = ((), (), s32[]{:S(2)}) async-start(), calls=%async_computation.5 | async-start | bytes 2621440 | tf_op jit(solution)/shard_map/all_gather | solution.py:65
  68.3 167.7 %all-reduce.2.cloned.1.call-start = ((), (), s32[]{:S(2)}) async-start(), calls=%async_computation.1 | async-start | bytes 4194304 | tf_op jit(solution)/shard_map/psum | solution.py:91
  106.8 6.1 %copy-start.1 = (f32[4,512,2048]{2,1,0:T(8,128)}, f32[4,512,2048]{2,1,0:T(8,128)S(1)}, u32[]{:S(2)}) copy-start(f32[4,512,2048]{2,1,0:T(8,128)S(1)} %get-tuple-element.152) | copy-start | bytes 50331652
  149.9 90.7 %copy-start.6 = (f32[2048]{0:T(1024)S(1)}, f32[2048]{0:T(1024)}, u32[]{:S(2)}) copy-start(f32[2048]{0:T(1024)} %param.17) | copy-start | bytes 24580
  149.9 150.1 %reduce-scatter.2.cloned.1.call-start = ((), (), s32[]{:S(2)}) async-start(), calls=%async_computation.2 | async-start | bytes 2621440 | tf_op jit(solution)/shard_map/reduce_scatter | solution.py:100
  240.6 17.9 %copy-start.3 = (f32[2048]{0:T(1024)S(1)}, f32[2048]{0:T(1024)}, u32[]{:S(2)}) copy-start(f32[2048]{0:T(1024)} %param.20) | copy-start | bytes 24580
  240.6 74.8 %copy-start.4 = (f32[2048]{0:T(1024)S(1)}, f32[2048]{0:T(1024)}, u32[]{:S(2)}) copy-start(f32[2048]{0:T(1024)} %param.21) | copy-start | bytes 24580
  257.2 70.5 %copy-start.2 = (f32[2048]{0:T(1024)S(1)}, f32[2048]{0:T(1024)}, u32[]{:S(2)}) copy-start(f32[2048]{0:T(1024)} %param.22) | copy-start | bytes 24580
Sparse Core Ops, SparseCore 0:
  9.6 47.5 all-gather.8
  67.7 33.8 all-gather.10
  103.4 35.0 all-gather.12
  150.0 85.9 all-reduce.1
  257.3 42.5 reduce-scatter.1
